TPU v7x, 32 devices: a whole 2x2x4 slice. The times are simulated.
32 devices in a mesh: seq: 2 (over x), tensor: 4 (over z), bucket: 4 (over y, core).
Axes of the slice: x: 2, y: 2, z: 4, core: 2. Of those that a mesh axis runs over, the one named last changes fastest.
Arguments:
- queries: bfloat16 [4, 1024, 3072], P('bucket', ('seq', 'tensor')), may hold values from -6 to 6
- keys: bfloat16 [4, 1024, 3072], P('bucket', ('seq', 'tensor')), may hold values from -6 to 6
- values: bfloat16 [4, 1024, 3072], P('bucket', ('seq', 'tensor')), may hold values from -6 to 6
- lengths: int32 [4], P('bucket'), may hold values from 256 to 1024, as said below
- out_weight: bfloat16 [3072, 3072], P(('seq', 'bucket'), 'tensor'), may hold values from -0.109375 to 0.109375
Outputs:
- projected: bfloat16 [4, 1024, 3072], P('bucket', ('seq', 'tensor'))
Inputs may be any that keep to these rules, and one draw needn't show every extreme that they name: `lengths`: each bucket has 256 to 1024 live tokens, and at least one bucket has all 1024.
All inputs are finite; a program needn't handle non-finite values.
Results may differ from a plain program's by a relative error of at most 0.018.
Values may be sent and summed in bfloat16 or wider, within the bound.
No kernel may reach another device: no remote copies, remote signals or barrier semaphores. Data moves between devices by JAX's collectives and lax.ppermute only.
A program may use at most 128 MiB of HBM per device.

v0:
```python
import jax
import jax.numpy as jnp
from jax import lax
from jax.sharding import PartitionSpec as P

HS = 128
MASKED_SCORE = -1e30


def shards(queries, keys, values, lengths, out_weight):
    tok_rows = queries.shape[1]
    n_tensor = lax.axis_size("tensor")
    tensor_index = lax.axis_index("tensor")
    live_len = lengths[0]
    local_q, local_k, local_v = (
        lax.all_to_all(queries[0], "seq", split_axis=1, concat_axis=0, tiled=True),
        lax.all_to_all(keys[0], "seq", split_axis=1, concat_axis=0, tiled=True),
        lax.all_to_all(values[0], "seq", split_axis=1, concat_axis=0, tiled=True),
    )
    row_count, col_count = local_q.shape
    head_count = col_count // HS
    query_heads = local_q.reshape(row_count, head_count, HS)

    def spots(first_row, total_rows):
        index_row = first_row + jnp.arange(total_rows, dtype=jnp.int32)
        owner = index_row // row_count
        within = index_row % row_count
        return (within // tok_rows * n_tensor + owner) * tok_rows + within % tok_rows

    query_usable = spots(tensor_index * row_count, row_count) < live_len
    initial = (
        jnp.full((row_count, head_count), MASKED_SCORE, jnp.float32),
        jnp.zeros((row_count, head_count), jnp.float32),
        jnp.zeros((row_count, head_count, HS), jnp.float32),
    )
    carried = initial
    first_row = jnp.int32(0)
    key_rows = lax.all_gather(local_k, "tensor", axis=0, tiled=True)
    value_rows = lax.all_gather(local_v, "tensor", axis=0, tiled=True)
    for offset in range(key_rows.shape[0] // row_count):
        row_peak, row_sum, accumulated = carried
        key_tile = key_rows[offset * row_count : (offset + 1) * row_count].reshape(
            row_count, head_count, HS
        )
        value_tile = value_rows[offset * row_count : (offset + 1) * row_count].reshape(
            row_count, head_count, HS
        )
        key_usable = spots(first_row + offset * row_count, row_count) < live_len
        scores = jnp.einsum(
            "qhd,khd->qhk", query_heads, key_tile, preferred_element_type=jnp.float32
        ) * HS ** (-0.5)
        scores = jnp.where(key_usable[None, None, :], scores, MASKED_SCORE)
        peak_new = jnp.maximum(row_peak, jnp.max(scores, axis=-1))
        exponent = jnp.where(key_usable[None, None, :], jnp.exp(scores - peak_new[..., None]), 0.0)
        rescale = jnp.exp(row_peak - peak_new)
        accumulated = accumulated * rescale[..., None] + jnp.einsum(
            "qhk,khd->qhd",
            exponent.astype(jnp.bfloat16),
            value_tile,
            preferred_element_type=jnp.float32,
        )
        carried = (peak_new, row_sum * rescale + jnp.sum(exponent, axis=-1), accumulated)
    row_peak, row_sum, accumulated = carried
    attended = accumulated / row_sum[..., None]
    mixed = jnp.where(query_usable[:, None], attended.reshape(row_count, col_count), 0.0).astype(
        jnp.bfloat16
    )
    restored = lax.all_to_all(mixed, "seq", split_axis=0, concat_axis=1, tiled=True)
    wide_weight = lax.all_gather(out_weight, "tensor", axis=1, tiled=True)
    summed = jnp.dot(
        restored,
        lax.all_gather(wide_weight, ("seq", "bucket"), axis=0, tiled=True),
        preferred_element_type=jnp.float32,
    )
    return summed.astype(jnp.bfloat16)[None]


def solution(mesh):
    in_specs = (
        P("bucket", ("seq", "tensor"), None),
        P("bucket", ("seq", "tensor"), None),
        P("bucket", ("seq", "tensor"), None),
        P("bucket"),
        P(("seq", "bucket"), "tensor"),
    )
    out_specs = P("bucket", ("seq", "tensor"), None)
    return jax.shard_map(shards, mesh=mesh, in_specs=in_specs, out_specs=out_specs, check_vma=False)
```

profile of v0, /device:TPU:0, one launch (start us, length us, event | category | flops | bytes accessed | tf_op | source)
XLA Modules:
  0.0 309.9 jit_solution(5005568359367810147)
XLA Ops:
  6.5 0.7 all-gather.9.cloned.1.call-update
  7.3 0.0 all-gather.5.cloned.1.call-start
  7.3 1.5 copy.68
  8.8 14.8 %all_to_all.70 = bf16[128,2,1536]{0,2,1:T(8,128)(2,1)S(1)} all-to-all(bf16[128,2,1536]{0,2,1:T(8,128)(2,1)S(1)} %bitcast.125), channel_id=1, replica_groups=mesh['seq'=2,'tensor'=4,'bucket'=4] {'seq'}, dimensions={1} | all-to-all | bytes 1572864 | tf_op jit(solution)/shard_map/all_to_all | solution.py:17
  23.6 1.2 copy.69
  24.8 0.0 all-gather.7.cloned.1.call-start
  24.9 0.4 copy.75
  25.3 12.5 %all_to_all.71 = bf16[128,2,1536]{0,2,1:T(8,128)(2,1)S(1)} all-to-all(bf16[128,2,1536]{0,2,1:T(8,128)(2,1)S(1)} %bitcast.126), channel_id=1, replica_groups=mesh['seq'=2,'tensor'=4,'bucket'=4] {'seq'}, dimensions={1} | all-to-all | bytes 1572864 | tf_op jit(solution)/shard_map/all_to_all | solution.py:18
  37.8 1.2 copy.76
  39.0 0.0 all-gather.11.cloned.1.call-start
  39.0 22.6 %all-gather.9.cloned.1.call-done = bf16[384,3072]{1,0:T(8,128)(2,1)} async-done(((bf16[384,768]{1,0:T(8,128)(2,1)}), bf16[384,3072]{1,0:T(8,128)(2,1)}) %all-gather.9.cloned.1.call-update) | async-done | bytes 2359312 | tf_op jit(solution)/shard_map/all_gather | solution.py:69
  61.6 0.0 all-gather.11.cloned.1.call-update
  61.7 1.2 copy.71
  62.8 3.5 %all-to-all-start.1 = ((bf16[128,2,1536]{0,2,1:T(8,128)(2,1)}), bf16[128,2,1536]{0,2,1:T(8,128)(2,1)S(1)}, u32[]{:S(2)}, u32[]{:S(2)}) async-start(bf16[128,2,1536]{0,2,1:T(8,128)(2,1)} %bitcast.5), calls=%async_computation.1 | async-start | bytes 1572864 | tf_op jit(solution)/shard_map/all_to_all | solution.py:16
  67.1 10.2 %all-to-all-done.1 = bf16[128,2,1536]{0,2,1:T(8,128)(2,1)S(1)} async-done(((bf16[128,2,1536]{0,2,1:T(8,128)(2,1)}), bf16[128,2,1536]{0,2,1:T(8,128)(2,1)S(1)}, u32[]{:S(2)}, u32[]{:S(2)}) %all-to-all-start.1) | async-done | bytes 786464 | tf_op jit(solution)/shard_map/all_to_all | solution.py:16
  77.3 6.7 %copy.72 = bf16[2,128,1536]{1,0,2:T(2,128)(2,1)S(1)} copy(bf16[2,128,1536]{1,2,0:T(8,128)(2,1)S(1)} %bitcast.122) | data formatting | bytes 1572864 | tf_op jit(solution)/shard_map/all_to_all | solution.py:16
  83.9 0.5 reshape.424
  84.4 41.0 %all-gather.5.cloned.1.call-done = bf16[1024,1536]{1,0:T(8,128)(2,1)} async-done(((bf16[256,1536]{1,0:T(8,128)(2,1)}), bf16[1024,1536]{1,0:T(8,128)(2,1)}) %all-gather.5.cloned.1.call-update) | async-done | bytes 3145744 | tf_op jit(solution)/shard_map/all_gather | solution.py:38
  125.4 2.9 fusion.89
  128.4 1.2 copy.70
  129.6 0.3 copy.92
  129.8 0.3 copy.86
  130.1 1.4 copy.80
  131.5 57.6 %all-gather.7.cloned.1.call-done = bf16[1024,1536]{1,0:T(8,128)(2,1)} async-done(((bf16[256,1536]{1,0:T(8,128)(2,1)}), bf16[1024,1536]{1,0:T(8,128)(2,1)}) %all-gather.7.cloned.1.call-update) | async-done | bytes 3145744 | tf_op jit(solution)/shard_map/all_gather | solution.py:39
  189.1 3.6 %fusion.88 = (bf16[256,1536]{1,0:T(8,128)(2,1)}, bf16[256,1536]{1,0:T(8,128)(2,1)}, bf16[256,1536]{1,0:T(8,128)(2,1)}, bf16[256,1536]{1,0:T(8,128)(2,1)}) fusion(bf16[1024,1536]{1,0:T(8,128)(2,1)} %all-gather.7.cloned.1.call-done), kind=kLoop, calls=%fused_computation.155 | loop fusion | bytes 6291456 | tf_op jit(solution)/shard_map/slice | solution.py:45
  192.7 2.3 copy.83
  195.0 2.5 copy.89
  197.5 2.4 copy.95
  199.9 2.5 copy.77
  202.4 1.9 bitcast_reduce_fusion.3
  204.3 0.8 bitcast_reduce_fusion
  205.2 0.8 bitcast_reduce_fusion.1
  206.1 0.8 bitcast_reduce_fusion.2
  206.9 0.8 fusion.11
  207.8 0.8 fusion.13
  208.6 0.8 fusion.15
  209.5 0.8 fusion.9
  210.4 1.2 fusion.21
  211.6 1.4 fusion.19
  212.9 1.2 fusion.17
  214.2 3.0 fusion.25
  217.2 0.3 copy.98
  217.5 0.2 reshape.432
  217.7 0.8 select_convert_fusion
  218.4 0.1 copy.99
  218.6 16.7 %all_to_all.72 = bf16[2,128,1536]{1,2,0:T(8,128)(2,1)S(1)} all-to-all(bf16[2,128,1536]{1,2,0:T(8,128)(2,1)S(1)} %copy.99), channel_id=1, replica_groups=mesh['seq'=2,'tensor'=4,'bucket'=4] {'seq'}, dimensions={0} | all-to-all | bytes 1572864 | tf_op jit(solution)/shard_map/all_to_all | solution.py:68
  235.3 58.3 %all-gather.11.cloned.1.call-done = bf16[3072,3072]{1,0:T(8,128)(2,1)} async-done(((bf16[384,3072]{1,0:T(8,128)(2,1)}), bf16[3072,3072]{1,0:T(8,128)(2,1)}) %all-gather.11.cloned.1.call-update) | async-done | bytes 18874384 | tf_op jit(solution)/shard_map/all_gather | solution.py:72
  293.5 9.9 %fusion = bf16[1,128,3072]{2,1,0:T(8,128)(2,1)} fusion(bf16[128,3072]{0,1:T(8,128)(2,1)S(1)} %bitcast.115, bf16[3072,3072]{1,0:T(8,128)(2,1)} %all-gather.11.cloned.1.call-done), kind=kOutput, calls=%fused_computation.1 | convolution fusion | flops 2416312320 | bytes 20447232 | tf_op jit(solution)/shard_map/dot_general | solution.py:70
  (20 shorter events, 0.2 us)
Async XLA Ops:
  6.5 18.3 %copy-start = (bf16[1,128,3072]{2,1,0:T(8,128)(2,1)S(1)}, bf16[1,128,3072]{2,1,0:T(8,128)(2,1)}, u32[]{:S(2)}) copy-start(bf16[1,128,3072]{2,1,0:T(8,128)(2,1)} %param.7) | copy-start | bytes 2359300
  6.5 55.1 %all-gather.9.cloned.1.call-start = ((), (), s32[]{:S(2)}) async-start(), calls=%async_computation.6 | async-start | bytes 2949120 | tf_op jit(solution)/shard_map/all_gather | solution.py:69
  7.3 118.2 %all-gather.5.cloned.1.call-start = ((), (), s32[]{:S(2)}) async-start(), calls=%async_computation.4 | async-start | bytes 3932160 | tf_op jit(solution)/shard_map/all_gather | solution.py:38
  24.8 164.3 %all-gather.7.cloned.1.call-start = ((), (), s32[]{:S(2)}) async-start(), calls=%async_computation.5 | async-start | bytes 3932160 | tf_op jit(solution)/shard_map/all_gather | solution.py:39
  25.3 36.4 %copy-start.1 = (bf16[1,128,3072]{2,1,0:T(8,128)(2,1)S(1)}, bf16[1,128,3072]{2,1,0:T(8,128)(2,1)}, u32[]{:S(2)}) copy-start(bf16[1,128,3072]{2,1,0:T(8,128)(2,1)} %param.5) | copy-start | bytes 2359300
  39.0 254.6 %all-gather.11.cloned.1.call-start = ((), (), s32[]{:S(2)}) async-start(), calls=%async_computation.7 | async-start | bytes 21233664 | tf_op jit(solution)/shard_map/all_gather | solution.py:72
  62.8 14.4 %all-to-all-start.1 = ((bf16[128,2,1536]{0,2,1:T(8,128)(2,1)}), bf16[128,2,1536]{0,2,1:T(8,128)(2,1)S(1)}, u32[]{:S(2)}, u32[]{:S(2)}) async-start(bf16[128,2,1536]{0,2,1:T(8,128)(2,1)} %bitcast.5), calls=%async_computation.1 | async-start | bytes 1572864 | tf_op jit(solution)/shard_map/all_to_all | solution.py:16
  208.6 1.7 copy-start.5
  210.4 1.2 copy-start.4
  211.6 1.4 copy-start.3
  212.9 1.2 copy-start.2
Sparse Core Ops, SparseCore 0:
  8.9 52.6 all-gather.8
  63.2 62.1 all-gather.4
  127.0 62.0 all-gather.6
  190.9 102.6 all-gather.10
where the time goes:
time: 311 us; the launch traced here: 310 us
  waiting for transfers between devices  190 us (61%)
  blocking collectives  44 us (14%)
  local copies, waits for them, and re-layouts  32.5 us (10%)
  matrix products  21.1 us (7%)
  between operations  14.1 us (5%)
  other arithmetic  4.22 us (1%)
  starting transfers between devices  3.66 us (1%)
    all_gather x1, waiting for transfers between devices, shards(): lax.all_gather(wide_weight, ('seq', 'bucket'), axis=0, tiled=True)  58.3 us
    all_gather x1, waiting for transfers between devices, shards(): value_rows = lax.all_gather(local_v, 'tensor', axis=0, tiled=True)  57.6 us
    all_gather x1, waiting for transfers between devices, shards(): key_rows = lax.all_gather(local_k, 'tensor', axis=0, tiled=True)  41 us
    all_gather x1, waiting for transfers between devices, shards(): wide_weight = lax.all_gather(out_weight, 'tensor', axis=1, tiled=True)  22.6 us
    all_to_all x1, blocking collectives, shards(): lax.all_to_all(mixed, 'seq', split_axis=0, concat_axis=1, tiled=True)  16.7 us
    all_to_all x1, blocking collectives, shards(): lax.all_to_all(keys[0], 'seq', split_axis=1, concat_axis=0, tiled=True)  14.8 us
    slice x5, local copies, waits for them, and re-layouts, shards(): value_rows[offset * row_count:(offset + 1) * row_count]  13.3 us
    all_to_all x1, blocking collectives, shards(): lax.all_to_all(values[0], 'seq', split_axis=1, concat_axis=0, tiled=True)  12.5 us
  transfers between devices with their start and end apart: 5, of which 5 were waited for; matrix products, arithmetic and copies ran while one was open for 15% of the time, Pallas kernels for 0%

commit v1 on v0

--- a/solution.py
+++ b/solution.py
@@ -36,7 +36,14 @@
     carried = initial
     first_row = jnp.int32(0)
     key_rows = lax.all_gather(local_k, "tensor", axis=0, tiled=True)
-    value_rows = lax.all_gather(local_v, "tensor", axis=0, tiled=True)
+    ring = [local_v]
+    for hop in range(3):
+        ring.append(lax.ppermute(ring[-1], "tensor", [(dev, (dev + 1) % 4) for dev in range(4)]))
+    value_rows = jnp.roll(
+        jnp.concatenate(ring[::-1], axis=0),
+        (lax.axis_index("tensor") + 1) * ring[0].shape[0],
+        axis=0,
+    )
     for offset in range(key_rows.shape[0] // row_count):
         row_peak, row_sum, accumulated = carried
         key_tile = key_rows[offset * row_count : (offset + 1) * row_count].reshape(

time: 311 us -> 285 us (0.916)
  waiting for transfers between devices: 190 us -> 153 us
  starting transfers between devices: 3.66 us -> 16.4 us
  blocking collectives: 44 us -> 50.6 us
  local copies, waits for them, and re-layouts: 32.5 us -> 28.1 us
    ppermute x0 -> x3, waiting for transfers between devices: none -> 70.4 us  [shards(): lax.ppermute(ring[-1], 'tensor', [(dev, (dev + 1) % 4) for dev in range(4)])]
    all_gather x1 -> x0, waiting for transfers between devices: 57.6 us -> none  [shards(): value_rows = lax.all_gather(local_v, 'tensor', axis=0, tiled=True)]
    all_gather x1, waiting for transfers between devices: 41 us -> 0.01 us  [shards(): key_rows = lax.all_gather(local_k, 'tensor', axis=0, tiled=True)]
    all_gather x1, waiting for transfers between devices: 58.3 us -> 25.5 us  [shards(): lax.all_gather(wide_weight, ('seq', 'bucket'), axis=0, tiled=True)]
    all_gather x1, waiting for transfers between devices: 22.6 us -> 36.6 us  [shards(): wide_weight = lax.all_gather(out_weight, 'tensor', axis=1, tiled=True)]
    ppermute x0 -> x3, starting transfers between devices: none -> 12.7 us  [shards(): lax.ppermute(ring[-1], 'tensor', [(dev, (dev + 1) % 4) for dev in range(4)])]
    slice x5 -> x1, local copies, waits for them, and re-layouts: 13.3 us -> 1.85 us  [shards(): value_rows[offset * row_count:(offset + 1) * row_count]]
    all_to_all x1, waiting for transfers between devices: 10.2 us -> 19.4 us  [shards(): lax.all_to_all(queries[0], 'seq', split_axis=1, concat_axis=0, tiled=True)]
  transfers between devices with their start and end apart: 5 -> 7, of which waited for: 5 -> 5; matrix products, arithmetic and copies ran while one was open for 15% -> 14% of each run, Pallas kernels for 0% -> 0%
where the time goes in v1:
time: 285 us; the launch traced here: 284 us
  waiting for transfers between devices  153 us (54%)
  blocking collectives  50.6 us (18%)
  local copies, waits for them, and re-layouts  28.1 us (10%)
  matrix products  18.9 us (7%)
  starting transfers between devices  16.4 us (6%)
  between operations  14.1 us (5%)
  other arithmetic  3.63 us (1%)
    ppermute x3, waiting for transfers between devices, shards(): lax.ppermute(ring[-1], 'tensor', [(dev, (dev + 1) % 4) for dev in range(4)])  70.4 us
    all_gather x1, waiting for transfers between devices, shards(): wide_weight = lax.all_gather(out_weight, 'tensor', axis=1, tiled=True)  36.6 us
    all_gather x1, waiting for transfers between devices, shards(): lax.all_gather(wide_weight, ('seq', 'bucket'), axis=0, tiled=True)  25.5 us
    all_to_all x1, blocking collectives, shards(): lax.all_to_all(mixed, 'seq', split_axis=0, concat_axis=1, tiled=True)  22.3 us
    all_to_all x1, waiting for transfers between devices, shards(): lax.all_to_all(queries[0], 'seq', split_axis=1, concat_axis=0, tiled=True)  19.4 us
    all_to_all x1, blocking collectives, shards(): lax.all_to_all(keys[0], 'seq', split_axis=1, concat_axis=0, tiled=True)  14.9 us
    all_to_all x1, blocking collectives, shards(): lax.all_to_all(values[0], 'seq', split_axis=1, concat_axis=0, tiled=True)  13.3 us
    ppermute x3, starting transfers between devices, shards(): lax.ppermute(ring[-1], 'tensor', [(dev, (dev + 1) % 4) for dev in range(4)])  12.7 us
  transfers between devices with their start and end apart: 7, of which 5 were waited for; matrix products, arithmetic and copies ran while one was open for 14% of the time, Pallas kernels for 0%

profile of v1, /device:TPU:0, one launch (start us, length us, event | category | flops | bytes accessed | tf_op | source)
XLA Modules:
  0.0 284.2 jit_solution(3437254395051684471)
XLA Ops:
  6.5 0.7 all-gather.6.cloned.1.call-update
  7.3 1.5 copy.75
  8.8 14.9 %all_to_all.70 = bf16[128,2,1536]{0,2,1:T(8,128)(2,1)S(1)} all-to-all(bf16[128,2,1536]{0,2,1:T(8,128)(2,1)S(1)} %bitcast.126), channel_id=1, replica_groups=mesh['seq'=2,'tensor'=4,'bucket'=4] {'seq'}, dimensions={1} | all-to-all | bytes 1572864 | tf_op jit(solution)/shard_map/all_to_all | solution.py:17
  23.8 1.2 copy.76
  25.1 36.6 %all-gather.6.cloned.1.call-done = bf16[384,3072]{1,0:T(8,128)(2,1)} async-done(((bf16[384,768]{1,0:T(8,128)(2,1)}), bf16[384,3072]{1,0:T(8,128)(2,1)}) %all-gather.6.cloned.1.call-update) | async-done | bytes 2359312 | tf_op jit(solution)/shard_map/all_gather | solution.py:76
  61.7 0.4 copy.82
  62.1 0.3 copy.83
  62.3 13.3 %all_to_all.71 = bf16[128,2,1536]{2,0,1:T(8,128)(2,1)S(1)} all-to-all(bf16[128,2,1536]{2,0,1:T(8,128)(2,1)S(1)} %copy.83), channel_id=1, replica_groups=mesh['seq'=2,'tensor'=4,'bucket'=4] {'seq'}, dimensions={1} | all-to-all | bytes 1572864 | tf_op jit(solution)/shard_map/all_to_all | solution.py:18
  75.7 0.3 copy.84
  76.0 38.4 %collective-permute-done = bf16[256,1536]{0,1:T(8,128)(2,1)S(1)} collective-permute-done((bf16[256,1536]{0,1:T(8,128)(2,1)S(1)}, bf16[256,1536]{0,1:T(8,128)(2,1)S(1)}, u32[]{:S(2)}, u32[]{:S(2)}) %collective-permute-start) | collective-permute-done | bytes 786464 | tf_op jit(solution)/shard_map/ppermute | solution.py:41
  114.4 12.6 %collective-permute-start.1 = (bf16[256,1536]{0,1:T(8,128)(2,1)S(1)}, bf16[256,1536]{0,1:T(8,128)(2,1)S(1)}, u32[]{:S(2)}, u32[]{:S(2)}) collective-permute-start(bf16[256,1536]{0,1:T(8,128)(2,1)S(1)} %collective-permute-done), channel_id=1, source_target_pairs={{0,4},{4,8},{8,12},{12,0},{1,5},{5,9},{9,13},{13,1},{2,6},{6,10},{... | collective-permute-start | bytes 2359304 | tf_op jit(solution)/shard_map/ppermute | solution.py:41
  127.0 32.0 %collective-permute-done.1 = bf16[256,1536]{0,1:T(8,128)(2,1)S(1)} collective-permute-done((bf16[256,1536]{0,1:T(8,128)(2,1)S(1)}, bf16[256,1536]{0,1:T(8,128)(2,1)S(1)}, u32[]{:S(2)}, u32[]{:S(2)}) %collective-permute-start.1) | collective-permute-done | bytes 786464 | tf_op jit(solution)/shard_map/ppermute | solution.py:41
  159.0 2.4 copy.78
  161.5 3.6 %all-to-all-start.1 = ((bf16[128,2,1536]{0,2,1:T(8,128)(2,1)}), bf16[128,2,1536]{0,2,1:T(8,128)(2,1)S(1)}, u32[]{:S(2)}, u32[]{:S(2)}) async-start(bf16[128,2,1536]{0,2,1:T(8,128)(2,1)} %bitcast.123), calls=%async_computation.1 | async-start | bytes 1572864 | tf_op jit(solution)/shard_map/all_to_all | solution.py:16
  165.8 19.4 %all-to-all-done.1 = bf16[128,2,1536]{0,2,1:T(8,128)(2,1)S(1)} async-done(((bf16[128,2,1536]{0,2,1:T(8,128)(2,1)}), bf16[128,2,1536]{0,2,1:T(8,128)(2,1)S(1)}, u32[]{:S(2)}, u32[]{:S(2)}) %all-to-all-start.1) | async-done | bytes 786464 | tf_op jit(solution)/shard_map/all_to_all | solution.py:16
  185.2 7.2 %copy.79 = bf16[2,128,1536]{1,0,2:T(2,128)(2,1)} copy(bf16[2,128,1536]{1,2,0:T(8,128)(2,1)S(1)} %bitcast.122) | data formatting | bytes 1572864 | tf_op jit(solution)/shard_map/all_to_all | solution.py:16
  192.4 2.6 reshape.424
  195.0 1.2 constant_dynamic-update-slice_fusion.7
  196.5 0.1 constant_dynamic-update-slice_fusion.4
  196.6 1.2 constant_dynamic-update-slice_fusion.3
  197.9 0.1 constant_dynamic-update-slice_fusion.2
  198.1 0.1 constant_dynamic-update-slice_fusion
  198.2 1.8 constant_dynamic-slice_fusion.3
  200.0 3.1 %fusion.89 = (bf16[256,1536]{1,0:T(8,128)(2,1)}, bf16[256,1536]{1,0:T(8,128)(2,1)S(1)}, bf16[256,1536]{1,0:T(8,128)(2,1)S(1)}, bf16[256,1536]{1,0:T(8,128)(2,1)S(1)}) fusion(bf16[1024,1536]{1,0:T(8,128)(2,1)} %all-gather.4.cloned.1.call-done), kind=kLoop, calls=%fused_computation.168 | loop fusion | bytes 6291456 | tf_op jit(solution)/shard_map/slice | solution.py:49
  203.1 1.2 copy.92
  204.3 0.3 copy.96
  204.6 0.3 copy.88
  204.8 1.6 copy.77
  206.5 2.2 bitcast_reduce_fusion.1
  208.7 0.9 bitcast_reduce_fusion
  209.5 0.9 bitcast_reduce_fusion.2
  210.4 0.9 bitcast_reduce_fusion.3
  211.3 0.8 fusion.15
  212.1 0.8 fusion.13
  213.0 0.8 fusion.11
  213.8 0.8 fusion.9
  214.7 0.9 fusion.19
  215.7 0.2 copy-done.3
  215.9 0.9 fusion.21
  216.8 0.2 copy-done.2
  217.0 0.9 fusion.23
  217.9 0.2 copy-done.1
  218.1 1.5 fusion.25
  219.6 0.2 reshape.432
  219.8 0.2 fusion.29
  220.0 22.3 %all_to_all.72 = bf16[2,128,1536]{1,2,0:T(8,128)(2,1)S(1)} all-to-all(bf16[2,128,1536]{1,2,0:T(8,128)(2,1)S(1)} %fusion.29), channel_id=1, replica_groups=mesh['seq'=2,'tensor'=4,'bucket'=4] {'seq'}, dimensions={0} | all-to-all | bytes 1572864 | tf_op jit(solution)/shard_map/all_to_all | solution.py:75
  242.3 25.5 %all-gather.8.cloned.1.call-done = bf16[3072,3072]{1,0:T(8,128)(2,1)} async-done(((bf16[384,3072]{1,0:T(8,128)(2,1)}), bf16[3072,3072]{1,0:T(8,128)(2,1)}) %all-gather.8.cloned.1.call-update) | async-done | bytes 18874384 | tf_op jit(solution)/shard_map/all_gather | solution.py:79
  267.8 9.9 %fusion = bf16[1,128,3072]{2,1,0:T(8,128)(2,1)} fusion(bf16[128,3072]{0,1:T(8,128)(2,1)S(1)} %bitcast.116, bf16[3072,3072]{1,0:T(8,128)(2,1)} %all-gather.8.cloned.1.call-done), kind=kOutput, calls=%fused_computation.1 | convolution fusion | flops 2416312320 | bytes 20447232 | tf_op jit(solution)/shard_map/dot_general | solution.py:77
  (24 shorter events, 0.6 us)
Async XLA Ops:
  6.5 55.1 %all-gather.6.cloned.1.call-start = ((), (), s32[]{:S(2)}) async-start(), calls=%async_computation.5 | async-start | bytes 2949120 | tf_op jit(solution)/shard_map/all_gather | solution.py:76
  7.3 192.8 %all-gather.4.cloned.1.call-start = ((), (), s32[]{:S(2)}) async-start(), calls=%async_computation.4 | async-start | bytes 3932160 | tf_op jit(solution)/shard_map/all_gather | solution.py:38
  8.8 52.9 %copy-start = (bf16[1,128,3072]{2,1,0:T(8,128)(2,1)S(1)}, bf16[1,128,3072]{2,1,0:T(8,128)(2,1)}, u32[]{:S(2)}) copy-start(bf16[1,128,3072]{2,1,0:T(8,128)(2,1)} %param.7) | copy-start | bytes 2359300
  25.0 242.8 %all-gather.8.cloned.1.call-start = ((), (), s32[]{:S(2)}) async-start(), calls=%async_computation.6 | async-start | bytes 21233664 | tf_op jit(solution)/shard_map/all_gather | solution.py:79
  75.9 38.5 %collective-permute-start = (bf16[256,1536]{0,1:T(8,128)(2,1)S(1)}, bf16[256,1536]{0,1:T(8,128)(2,1)S(1)}, u32[]{:S(2)}, u32[]{:S(2)}) collective-permute-start(bf16[256,1536]{0,1:T(8,128)(2,1)S(1)} %copy.84), channel_id=1, source_target_pairs={{0,4},{4,8},{8,12},{12,0},{1,5},{5,9},{9,13},{13,1},{2,6},{6,10},{... | collective-permute-start | bytes 2359304 | tf_op jit(solution)/shard_map/ppermute | solution.py:41
  114.4 44.6 %collective-permute-start.1 = (bf16[256,1536]{0,1:T(8,128)(2,1)S(1)}, bf16[256,1536]{0,1:T(8,128)(2,1)S(1)}, u32[]{:S(2)}, u32[]{:S(2)}) collective-permute-start(bf16[256,1536]{0,1:T(8,128)(2,1)S(1)} %collective-permute-done), channel_id=1, source_target_pairs={{0,4},{4,8},{8,12},{12,0},{1,5},{5,9},{9,13},{13,1},{2,6},{6,10},{... | collective-permute-start | bytes 2359304 | tf_op jit(solution)/shard_map/ppermute | solution.py:41
  159.0 36.0 %collective-permute-start.2 = (bf16[256,1536]{0,1:T(8,128)(2,1)S(1)}, bf16[256,1536]{0,1:T(8,128)(2,1)}, u32[]{:S(2)}, u32[]{:S(2)}) collective-permute-start(bf16[256,1536]{0,1:T(8,128)(2,1)S(1)} %collective-permute-done.1), channel_id=1, source_target_pairs={{0,4},{4,8},{8,12},{12,0},{1,5},{5,9},{9,13},{13,1},{2,6},{6,10},{... | collective-permute-start | bytes 2359304 | tf_op jit(solution)/shard_map/ppermute | solution.py:41
  161.5 23.7 %all-to-all-start.1 = ((bf16[128,2,1536]{0,2,1:T(8,128)(2,1)}), bf16[128,2,1536]{0,2,1:T(8,128)(2,1)S(1)}, u32[]{:S(2)}, u32[]{:S(2)}) async-start(bf16[128,2,1536]{0,2,1:T(8,128)(2,1)} %bitcast.123), calls=%async_computation.1 | async-start | bytes 1572864 | tf_op jit(solution)/shard_map/all_to_all | solution.py:16
  213.0 1.7 copy-start.4
  214.7 1.1 copy-start.3
  215.9 1.1 copy-start.2
  217.0 1.1 copy-start.1
Sparse Core Ops, SparseCore 0:
  8.9 52.6 all-gather.5
  63.2 88.6 all-gather.3
  153.8 113.9 all-gather.7
